TPU v7x, 32 devices: a whole 2x2x4 slice. The times are simulated.
32 devices in a mesh: ta: 2 (over x), gz: 4 (over y, core), gy: 4 (over z).
Axes of the slice: x: 2, y: 2, z: 4, core: 2. Of those that a mesh axis runs over, the one named last changes fastest.
Arguments:
- propagator: bfloat16 [2, 4, 3, 12, 2, 4, 512], P(None, None, None, None, 'ta', 'gz', 'gy'), may hold values from -6 to 6
- links: bfloat16 [2, 3, 3, 2, 4, 512], P(None, None, None, 'ta', 'gz', 'gy'), may hold values from -2.5 to 2.5
- source_z: int32 [2, 4], replicated, may hold values from 0 to 3
- displacements: int32 [3], replicated, may hold values from 0 to 2, each once
- momenta: int32 [4], replicated, may hold values from 1 to 3
- gamma_perm: int32 [4, 4], replicated, may hold values from 0 to 3, each once within a row
- gamma_phase: int32 [4, 4], replicated, may hold values from 0 to 3
Outputs:
- correlator: float32 [2, 3, 4, 4, 2], replicated
Inputs may be any that keep to these rules, and one draw needn't show every extreme that they name: `displacements`: every displacement from -1 to 1 appears exactly once. `gamma_perm`: each row is a permutation of the four spin indices.
All inputs are finite; a program needn't handle non-finite values.
Results may differ from a plain program's by a relative error of at most 0.0003.
Values may be sent and summed in bfloat16 or wider, within the bound.
A program may use at most 64 MiB of HBM per device.

v0:
```python
import math

import jax
import jax.numpy as jnp
from jax import lax
from jax.sharding import PartitionSpec as P

highest = lax.Precision.HIGHEST


def from_behind(array, axis, by):
    peers = lax.axis_size(axis)
    return lax.ppermute(array, axis, [(i, (i + by) % peers) for i in range(peers)])


def colour_apply(wilson, field_now):
    left_real = wilson[0][None, :, :, None, :]
    left_imag = wilson[1][None, :, :, None, :]
    right_real = field_now[0][:, None, :, :, :]
    right_imag = field_now[1][:, None, :, :, :]
    real_part = jnp.sum(left_real * right_real - left_imag * right_imag, axis=2)
    imag_part = jnp.sum(left_real * right_imag + left_imag * right_real, axis=2)
    return jnp.stack([real_part, imag_part])


def link_product(left_link, right_link):
    left_real = left_link[0][:, :, None, :]
    left_imag = left_link[1][:, :, None, :]
    right_real = right_link[0][None, :, :, :]
    right_imag = right_link[1][None, :, :, :]
    real_part = jnp.sum(left_real * right_real - left_imag * right_imag, axis=1)
    imag_part = jnp.sum(left_real * right_imag + left_imag * right_real, axis=1)
    return jnp.stack([real_part, imag_part])


def spin_pairs(source, field_now):
    source_real = source[0][:, None]
    source_imag = source[1][:, None]
    field_real = field_now[0][None]
    field_imag = field_now[1][None]
    real_part = jnp.sum(source_real * field_real + source_imag * field_imag, axis=(2, 3))
    imag_part = jnp.sum(source_real * field_imag - source_imag * field_real, axis=(2, 3))
    return (real_part, imag_part)


def site_traces(gamma_real, gamma_imag, pairs):
    pair_real, pair_imag = pairs
    table_real = gamma_real[:, :, :, None]
    table_imag = gamma_imag[:, :, :, None]
    real_part = jnp.sum(table_real * pair_real[None] - table_imag * pair_imag[None], axis=(1, 2))
    imag_part = jnp.sum(table_real * pair_imag[None] + table_imag * pair_real[None], axis=(1, 2))
    return (real_part, imag_part)


def gamma_tables(gamma_perm, gamma_phase):
    columns = jnp.arange(4, dtype=jnp.int32)
    hits = (gamma_perm[:, :, None] == columns[None, None, :]).astype(jnp.float32)
    real_part = (gamma_phase == 0).astype(jnp.float32) - (gamma_phase == 2).astype(jnp.float32)
    imag_part = (gamma_phase == 1).astype(jnp.float32) - (gamma_phase == 3).astype(jnp.float32)
    return (hits * real_part[:, :, None], hits * imag_part[:, :, None])


def body(propagator, links, source_z, displacements, momenta, gamma_perm, gamma_phase):
    gamma_real, gamma_imag = gamma_tables(gamma_perm, gamma_phase)
    adjoint_real = jnp.swapaxes(gamma_real, 1, 2)
    adjoint_imag = -jnp.swapaxes(gamma_imag, 1, 2)
    depth_count = lax.axis_size("gz")
    nsteps = (displacements.shape[0] - 1) // 2
    slices_dev = propagator.shape[4]
    sites_dev = propagator.shape[6]
    slices_all = slices_dev * lax.axis_size("ta")
    sites_total = sites_dev * lax.axis_size("gy") * depth_count
    scaling = 1.0 / (24.0 * math.sqrt(sites_total))
    field_data, link_data = (propagator, links)
    depth_local = 1
    depth_start = lax.axis_index("gz")
    block_sites = field_data.shape[-1]
    line_length = depth_local * block_sites
    flat_length = slices_dev * line_length
    field_flat = jnp.reshape(field_data, (2, 4, 3, 12, flat_length))
    links_flat = jnp.reshape(link_data, (2, 3, 3, flat_length))
    positions = jnp.arange(flat_length, dtype=jnp.int32)
    depth_flat = depth_start + positions // block_sites % depth_local
    slice_flat = lax.axis_index("ta") * slices_dev + positions // line_length
    slice_ids = jnp.arange(slices_all, dtype=jnp.int32)
    slice_hits = slice_ids[:, None] == slice_flat[None, :]
    source_flat = jnp.sum(jnp.where(slice_hits[:, None, :], source_z[:, :, None], 0), axis=0)
    turn_count = momenta[:, None] * (depth_flat[None, :] - source_flat) % depth_count
    angles = turn_count.astype(jnp.float32) * (2.0 * math.pi / depth_count)
    cosine = jnp.cos(angles)
    sine_table = jnp.sin(angles)
    slice_weight = slice_hits.astype(jnp.float32)

    def contract(trace, table):
        return jnp.einsum("tl,gl,pl->tgp", slice_weight, trace, table, precision=highest)

    def project(traces):
        trace_real, trace_imag = traces
        real_part = contract(trace_real, cosine) + contract(trace_imag, sine_table)
        imag_part = contract(trace_imag, cosine) - contract(trace_real, sine_table)
        return jnp.stack([real_part, imag_part], axis=-1) * scaling

    source = field_flat.astype(jnp.float32)
    unit = jnp.broadcast_to(jnp.eye(3, dtype=jnp.float32)[:, :, None], (3, 3, flat_length))
    identity = jnp.stack([unit, jnp.zeros_like(unit)])
    results = {0: project(site_traces(gamma_real, gamma_imag, spin_pairs(source, source)))}
    wilson = identity
    moved_field = field_flat
    moved_links = links_flat
    for reach in range(1, nsteps + 1):
        wilson = link_product(wilson, moved_links.astype(jnp.float32))
        moved_field, moved_links = from_behind((moved_field, moved_links), "gz", -1)
        pairs = spin_pairs(source, colour_apply(wilson, moved_field.astype(jnp.float32)))
        results[reach] = project(site_traces(gamma_real, gamma_imag, pairs))
        mirrored_trace_real, mirrored_trace_imag = site_traces(adjoint_real, adjoint_imag, pairs)
        other_real = contract(mirrored_trace_real, cosine) - contract(
            mirrored_trace_imag, sine_table
        )
        other_imag = contract(mirrored_trace_imag, cosine) + contract(
            mirrored_trace_real, sine_table
        )
        shift_turn = momenta * reach % depth_count
        shift_angle = shift_turn.astype(jnp.float32) * (2.0 * math.pi / depth_count)
        shift_cos = jnp.cos(shift_angle)
        shift_sin = jnp.sin(shift_angle)
        mirrored_real_part = other_real * shift_cos - other_imag * shift_sin
        mirrored_imag_part = -other_imag * shift_cos - other_real * shift_sin
        results[-reach] = jnp.stack([mirrored_real_part, mirrored_imag_part], axis=-1) * scaling
    stacked = jnp.stack([results[offset] for offset in range(-nsteps, nsteps + 1)], axis=1)
    offsets = jnp.arange(2 * nsteps + 1, dtype=jnp.int32)
    select = (displacements[:, None] == offsets[None, :]).astype(jnp.float32)
    ordered = jnp.einsum("jl,tlgpc->tjgpc", select, stacked, precision=highest)
    return lax.psum(ordered, ("ta", "gz", "gy"))


def solution(mesh):
    placed = (
        P(None, None, None, None, "ta", "gz", "gy"),
        P(None, None, None, "ta", "gz", "gy"),
        P(),
        P(),
        P(),
        P(),
        P(),
    )
    return jax.shard_map(body, mesh=mesh, in_specs=placed, out_specs=P(), check_vma=False)
```

profile of v0, /device:TPU:0, one launch (start us, length us, event | category | flops | bytes accessed | tf_op | source)
XLA Modules:
  0.0 51.4 jit_solution(15262922463979435672)
XLA Ops:
  0.0 2.4 %collective-permute-start = (bf16[2,4,3,12,128]{4,1,3,2,0:T(4,128)(2,1)}, bf16[2,4,3,12,128]{4,1,3,2,0:T(4,128)(2,1)S(1)}, u32[]{:S(2)}, u32[]{:S(2)}) collective-permute-start(bf16[2,4,3,12,128]{4,1,3,2,0:T(4,128)(2,1)} %bitcast.123), channel_id=1, source_target_pairs={{0,12},{4,0},{8,4},{12,8},{1,13},{5,1},{9,5},{13,9},{2,14},{6,2},{... | collective-permute-start | bytes 221192 | tf_op jit(solution)/shard_map/ppermute | solution.py:13
  2.4 0.7 %copy_convert_fusion = f32[2,3,3,1,1,128]{5,2,1,4,3,0:T(4,128)S(1)} fusion(bf16[2,3,3,1,1,128]{5,0,4,3,2,1:T(2,128)(2,1)} %param.8), kind=kLoop, calls=%fused_computation.41 | loop fusion | flops 2304 | bytes 13824 | tf_op jit(solution)/shard_map/convert_element_type | solution.py:111
  3.1 0.9 %bitcast_convert_fusion = f32[2,4,3,12,128]{4,1,3,2,0:T(4,128)S(1)} fusion(bf16[2,4,3,12,1,1,128]{6,1,5,4,3,2,0:T(4,128)(2,1)} %param.7), kind=kLoop, calls=%fused_computation.140 | loop fusion | flops 36864 | bytes 221184 | tf_op jit(solution)/shard_map/convert_element_type | solution.py:103
  4.1 0.0 copy-start.1
  4.1 0.7 %copy-done.1 = s32[4,4]{1,0:T(4,128)S(1)} copy-done((s32[4,4]{1,0:T(4,128)S(1)}, s32[4,4]{1,0:T(4,128)}, u32[]{:S(2)}) %copy-start.1) | copy-done | bytes 88
  4.8 0.0 copy-start.3
  4.8 0.6 %copy-done.3 = s32[4]{0:T(128)S(1)} copy-done((s32[4]{0:T(128)S(1)}, s32[4]{0:T(128)}, u32[]{:S(2)}) %copy-start.3) | copy-done | bytes 40
  5.5 0.7 %copy-done.2 = s32[2,4]{1,0:T(2,128)S(1)} copy-done((s32[2,4]{1,0:T(2,128)S(1)}, s32[2,4]{1,0:T(2,128)}, u32[]{:S(2)}) %copy-start.2) | copy-done | bytes 56
  6.2 0.1 select_reduce_fusion
  6.3 0.1 fusion.88
  6.5 0.7 %copy-done = s32[4,4]{1,0:T(4,128)S(1)} copy-done((s32[4,4]{1,0:T(4,128)S(1)}, s32[4,4]{1,0:T(4,128)}, u32[]{:S(2)}) %copy-start) | copy-done | bytes 88
  7.2 0.1 fusion.6
  7.2 0.1 subtract_reduce_fusion.6
  7.4 0.2 subtract_reduce_fusion.2
  7.6 0.4 add_reduce_fusion
  8.0 0.2 add_reduce_fusion.5
  8.1 0.2 fusion.24
  8.3 0.2 fusion.18
  8.5 0.2 convolution_add_fusion.1
  8.6 0.2 convolution_subtract_fusion.1
  8.8 0.2 fusion.34
  9.0 0.2 fusion.28
  9.1 0.2 convolution_subtract_fusion.2
  9.3 0.2 fusion.14
  9.4 0.2 fusion.8
  9.6 0.2 convolution_add_fusion
  9.8 0.2 convolution_subtract_fusion
  10.0 0.2 multiply_subtract_fusion.1
  10.2 0.6 %copy-done.4 = s32[3]{0:T(128)S(1)} copy-done((s32[3]{0:T(128)S(1)}, s32[3]{0:T(128)}, u32[]{:S(2)}) %copy-start.4) | copy-done | bytes 36
  10.8 0.2 convolution_bitcast_fusion
  11.1 39.7 %psum.7 = f32[2,3,4,4,2]{3,1,4,2,0:T(4,128)S(1)} all-reduce(f32[2,3,4,4,2]{3,1,4,2,0:T(4,128)S(1)} %convolution_bitcast_fusion), channel_id=1, replica_groups=mesh['ta'=2,'gz'=4,'gy'=4] {'ta','gz','gy'}, use_global_device_ids=true, to_apply=%region_15.16 | all-reduce | flops 192 | bytes 1536 | tf_op jit(solution)/shard_map/psum | solution.py:133
  50.8 0.6 %copy.45 = f32[2,3,4,4,2]{3,4,2,1,0:T(2,128)} copy(f32[2,3,4,4,2]{3,1,4,2,0:T(4,128)S(1)} %psum.7) | data formatting | bytes 1536 | tf_op jit(solution)/shard_map/psum | solution.py:133
  (20 shorter events, 0.3 us)
Async XLA Ops:
  0.0 7.3 %collective-permute-start = (bf16[2,4,3,12,128]{4,1,3,2,0:T(4,128)(2,1)}, bf16[2,4,3,12,128]{4,1,3,2,0:T(4,128)(2,1)S(1)}, u32[]{:S(2)}, u32[]{:S(2)}) collective-permute-start(bf16[2,4,3,12,128]{4,1,3,2,0:T(4,128)(2,1)} %bitcast.123), channel_id=1, source_target_pairs={{0,12},{4,0},{8,4},{12,8},{1,13},{5,1},{9,5},{13,9},{2,14},{6,2},{... | collective-permute-start | bytes 221192 | tf_op jit(solution)/shard_map/ppermute | solution.py:13
  4.1 0.7 %copy-start.1 = (s32[4,4]{1,0:T(4,128)S(1)}, s32[4,4]{1,0:T(4,128)}, u32[]{:S(2)}) copy-start(s32[4,4]{1,0:T(4,128)} %param.13) | copy-start | bytes 196
  4.8 0.7 %copy-start.3 = (s32[4]{0:T(128)S(1)}, s32[4]{0:T(128)}, u32[]{:S(2)}) copy-start(s32[4]{0:T(128)} %param.11) | copy-start | bytes 52
  5.5 0.7 %copy-start.2 = (s32[2,4]{1,0:T(2,128)S(1)}, s32[2,4]{1,0:T(2,128)}, u32[]{:S(2)}) copy-start(s32[2,4]{1,0:T(2,128)} %param.9) | copy-start | bytes 100
  6.5 0.7 %copy-start = (s32[4,4]{1,0:T(4,128)S(1)}, s32[4,4]{1,0:T(4,128)}, u32[]{:S(2)}) copy-start(s32[4,4]{1,0:T(4,128)} %param.12) | copy-start | bytes 196
  10.2 0.7 %copy-start.4 = (s32[3]{0:T(128)S(1)}, s32[3]{0:T(128)}, u32[]{:S(2)}) copy-start(s32[3]{0:T(128)} %param.10) | copy-start | bytes 40
where the time goes:
time: 51.7 us; the launch traced here: 51.4 us
  blocking collectives  39.7 us (77%)
  local copies, waits for them, and re-layouts  4.07 us (8%)
  other arithmetic  2.84 us (5%)
  starting transfers between devices  2.43 us (5%)
  matrix products  2.18 us (4%)
    psum x1, blocking collectives, body(): return lax.psum(ordered, ('ta', 'gz', 'gy'))  39.7 us
    unnamed x10, local copies, waits for them, and re-layouts  3.31 us
    ppermute x1, starting transfers between devices, from_behind(): lax.ppermute(array, axis, [(i, (i + by) % peers) for i in range(peers)])  2.43 us
    dot_general x12, matrix products, contract(): jnp.einsum('tl,gl,pl->tgp', slice_weight, trace, table, precision=highest)  1.96 us
  transfers between devices with their start and end apart: 1, of which 0 were waited for; matrix products, arithmetic and copies ran while one was open for 4% of the time, Pallas kernels for 0%

commit v1 on v0

v1 whole, which is shorter than its diff:
```python
import functools
import math

import jax
import jax.numpy as jnp
from jax import lax
from jax.experimental import pallas as pl
from jax.experimental.pallas import tpu as pltpu
from jax.sharding import PartitionSpec as P

MESH = pl.DeviceIdType.MESH
LANES = 128


def weights(lane_row, sizes, smem, place, scaling):
    ndisp, ng, np_, nz = sizes
    src, disp, mom, perm, phase = smem
    slice_at, depth_at = place
    nsteps = (ndisp - 1) // 2
    shape = (32, LANES)
    lane = lax.broadcasted_iota(jnp.int32, shape, 1) + lane_row * LANES
    row = lax.broadcasted_iota(jnp.int32, shape, 0)
    momentum = lane & (np_ - 1)
    out_part = (lane // np_) & 1
    gamma = (lane // (2 * np_)) & (ng - 1)
    entry = lane // (2 * np_ * ng)
    in_part = row // 16
    first = (row // 4) & 3
    second = row & 3
    reach = jnp.full(shape, 2 * nsteps + 1, jnp.int32)
    for j in range(ndisp):
        reach = jnp.where(entry == j, disp[j] - nsteps, reach)
    backward = reach < 0
    momenta = jnp.zeros(shape, jnp.int32)
    source = jnp.zeros(shape, jnp.int32)
    for p in range(np_):
        momenta = jnp.where(momentum == p, mom[p], momenta)
        source = jnp.where(momentum == p, src[slice_at, p], source)
    depth = depth_at - jnp.where(backward, reach, 0)
    turns = (momenta * (depth - source)).astype(jnp.float32) * (1.0 / nz)
    angle = (turns - jnp.floor(turns)) * (2.0 * math.pi)
    cosine = jnp.cos(angle)
    sine = jnp.sin(angle)
    sink = jnp.where(backward, second, first)
    other = jnp.where(backward, first, second)
    column = jnp.zeros(shape, jnp.int32)
    power = jnp.zeros(shape, jnp.int32)
    for g in range(ng):
        for s in range(4):
            here = (gamma == g) & (sink == s)
            column = jnp.where(here, perm[g, s], column)
            power = jnp.where(here, phase[g, s], power)
    quarter = power - out_part + jnp.where(backward, -in_part, in_part)
    quarter = quarter & 3
    value = jnp.where((quarter & 1) == 0, cosine, sine)
    value = jnp.where(quarter >= 2, -value, value)
    value = jnp.where((column == other) & (entry < ndisp), value * scaling, 0.0)
    return value, jnp.abs(reach)


def pair_sums(left, right, rows):
    half = rows // 2
    per = half // 4
    lefts = []
    turned = []
    rights = []
    for s in range(4):
        lefts.append(left[pl.ds(s, 2 * per, stride=4), :])
        rights.append(right[pl.ds(s, 2 * per, stride=4), :])
        turned.append(
            jnp.concatenate(
                [-left[pl.ds(half + s, per, stride=4), :], left[pl.ds(s, per, stride=4), :]],
                axis=0,
            )
        )
    out = []
    for group in (lefts, turned):
        for s in range(4):
            for u in range(4):
                product = (group[s] * rights[u]).reshape(2 * per // 8, 8, LANES)
                out.append(jnp.sum(jnp.sum(product, axis=0), axis=0, keepdims=True))
    stacked = jnp.concatenate(out, axis=0)
    return jnp.sum(stacked, axis=1, keepdims=True)


def kernel(
    sizes, scaling, ranks,
    prop, links, src_h, disp_h, mom_h, perm_h, phase_h,
    out,
    near, near_links, far, far_links, left, right,
    src, disp, mom, perm, phase,
    stage1, stage2,
    local_sem, s_send, s_recv, u_send, u_recv, a_send, a_recv, b_send, b_recv,
):
    ndisp, ng, np_, nz = sizes
    nta, ngz, ngy = ranks
    nsteps = (ndisp - 1) // 2
    rows = near.shape[0]
    part_rows = rows // 2
    colour_rows = part_rows // 3
    lane_rows = stage1.shape[1]
    ta, gz, gy = lax.axis_index("ta"), lax.axis_index("gz"), lax.axis_index("gy")

    loads = [
        pltpu.make_async_copy(a, b, local_sem.at[i])
        for i, (a, b) in enumerate(
            [(prop, near), (links, near_links), (src_h, src), (disp_h, disp),
             (mom_h, mom), (perm_h, perm), (phase_h, phase)]
        )
    ]
    for load in loads:
        load.start()

    barrier = pltpu.get_barrier_semaphore()
    peers1 = [(ta, lax.rem(gz + d, ngz), gy) for d in range(1, ngz)]
    peers2 = [
        (lax.rem(ta + i, nta), gz, lax.rem(gy + j, ngy))
        for i in range(nta) for j in range(ngy) if i + j
    ]
    for peer in peers1 + peers2:
        pl.semaphore_signal(barrier, inc=1, device_id=peer, device_id_type=MESH)
    pl.semaphore_wait(barrier, len(peers1) + len(peers2))

    loads[0].wait()
    loads[1].wait()
    sends = []
    for k in range(1, nsteps + 1):
        target = (ta, lax.rem(gz + ngz - k, ngz), gy)
        sends.append(pltpu.make_async_remote_copy(
            src_ref=near, dst_ref=far.at[k - 1], send_sem=s_send.at[k - 1],
            recv_sem=s_recv.at[k - 1], device_id=target, device_id_type=MESH))
        sends[-1].start()
    link_sends = []
    for k in range(1, nsteps):
        target = (ta, lax.rem(gz + ngz - k, ngz), gy)
        link_sends.append(pltpu.make_async_remote_copy(
            src_ref=near_links, dst_ref=far_links.at[k - 1], send_sem=u_send.at[k - 1],
            recv_sem=u_recv.at[k - 1], device_id=target, device_id_type=MESH))
        link_sends[-1].start()

    for load in loads[2:]:
        load.wait()
    left[...] = near[...].astype(jnp.float32)
    sums = [pair_sums(left, left, rows)]
    tables = [
        weights(h, sizes, (src, disp, mom, perm, phase), (ta, gz), scaling)
        for h in range(lane_rows)
    ]

    def link_at(ref):
        return [
            [
                [jnp.broadcast_to(ref[3 * a + b, pl.ds(part, 1), :].astype(jnp.float32), (8, LANES))
                 for part in range(2)]
                for b in range(3)
            ]
            for a in range(3)
        ]

    wilson = None
    for k in range(1, nsteps + 1):
        if k == 1:
            wilson = link_at(near_links)
        else:
            link_sends[k - 2].wait_recv()
            step = link_at(far_links.at[k - 2])
            wilson = [
                [
                    [
                        sum(wilson[a][c][0] * step[c][b][0] - wilson[a][c][1] * step[c][b][1] for c in range(3)),
                        sum(wilson[a][c][0] * step[c][b][1] + wilson[a][c][1] * step[c][b][0] for c in range(3)),
                    ]
                    for b in range(3)
                ]
                for a in range(3)
            ]
        sends[k - 1].wait_recv()
        for chunk in range(colour_rows // 16):
            field = [
                [
                    far[k - 1, pl.ds(part * part_rows + b * colour_rows + chunk * 16, 16), :]
                    .astype(jnp.float32).reshape(2, 8, LANES)
                    for b in range(3)
                ]
                for part in range(2)
            ]
            for a in range(3):
                real = sum(wilson[a][b][0] * field[0][b] - wilson[a][b][1] * field[1][b] for b in range(3))
                imag = sum(wilson[a][b][0] * field[1][b] + wilson[a][b][1] * field[0][b] for b in range(3))
                at = a * colour_rows + chunk * 16
                right[pl.ds(at, 16), :] = real.reshape(16, LANES)
                right[pl.ds(part_rows + at, 16), :] = imag.reshape(16, LANES)
        sums.append(pair_sums(left, right, rows))

    for h in range(lane_rows):
        table, reach = tables[h]
        chosen = jnp.zeros(table.shape, jnp.float32)
        for k in range(nsteps + 1):
            chosen = jnp.where(reach == k, sums[k], chosen)
        stage1[gz, pl.ds(h, 1), :] = jnp.sum(chosen * table, axis=0, keepdims=True)

    first = []
    for d in range(1, ngz):
        first.append(pltpu.make_async_remote_copy(
            src_ref=stage1.at[gz], dst_ref=stage1.at[gz], send_sem=a_send.at[d],
            recv_sem=a_recv.at[d], device_id=peers1[d - 1], device_id_type=MESH))
        first[-1].start()
    for copy in first:
        copy.wait_recv()
    total = stage1[0]
    for d in range(1, ngz):
        total = total + stage1[d]
    stage2[ta, gy] = total
    second = []
    for d, peer in enumerate(peers2):
        second.append(pltpu.make_async_remote_copy(
            src_ref=stage2.at[ta, gy], dst_ref=stage2.at[ta, gy], send_sem=b_send.at[d],
            recv_sem=b_recv.at[d], device_id=peer, device_id_type=MESH))
        second[-1].start()
    for copy in second:
        copy.wait_recv()
    for t in range(nta):
        total = stage2[t, 0]
        for d in range(1, ngy):
            total = total + stage2[t, d]
        out[t] = total
    for copy in sends + link_sends + first + second:
        copy.wait_send()


def body(ranks, propagator, links, source_z, displacements, momenta, gamma_perm, gamma_phase):
    nta, ngz, ngy = ranks
    sites = propagator.shape[6]
    ndisp, np_, ng = displacements.shape[0], momenta.shape[0], gamma_perm.shape[0]
    nsteps = (ndisp - 1) // 2
    sizes = (ndisp, ng, np_, ngz)
    scaling = 1.0 / (24.0 * math.sqrt(sites * ngy * ngz))
    field = jnp.transpose(propagator, (0, 2, 3, 4, 5, 1, 6)).reshape(-1, sites)
    link = jnp.transpose(links, (1, 2, 3, 4, 0, 5)).reshape(9, 2, sites)
    rows = field.shape[0]
    lane_rows = -(-ndisp * ng * np_ * 2 // LANES)
    more = max(nsteps - 1, 1)
    dma = pltpu.SemaphoreType.DMA
    reduced = pl.pallas_call(
        functools.partial(kernel, sizes, scaling, ranks),
        out_shape=jax.ShapeDtypeStruct((nta, lane_rows, LANES), jnp.float32),
        in_specs=[pl.BlockSpec(memory_space=pl.ANY)] * 7,
        out_specs=pl.BlockSpec(memory_space=pltpu.VMEM),
        scratch_shapes=[
            pltpu.VMEM((rows, sites), jnp.bfloat16),
            pltpu.VMEM((9, 2, sites), jnp.bfloat16),
            pltpu.VMEM((nsteps, rows, sites), jnp.bfloat16),
            pltpu.VMEM((more, 9, 2, sites), jnp.bfloat16),
            pltpu.VMEM((rows, sites), jnp.float32),
            pltpu.VMEM((rows, sites), jnp.float32),
            pltpu.SMEM(source_z.shape, jnp.int32),
            pltpu.SMEM(displacements.shape, jnp.int32),
            pltpu.SMEM(momenta.shape, jnp.int32),
            pltpu.SMEM(gamma_perm.shape, jnp.int32),
            pltpu.SMEM(gamma_phase.shape, jnp.int32),
            pltpu.VMEM((ngz, lane_rows, LANES), jnp.float32),
            pltpu.VMEM((nta, ngy, lane_rows, LANES), jnp.float32),
            dma((7,)), dma((nsteps,)), dma((nsteps,)), dma((more,)), dma((more,)),
            dma((ngz,)), dma((ngz,)), dma((nta * ngy,)), dma((nta * ngy,)),
        ],
        compiler_params=pltpu.CompilerParams(collective_id=0, has_side_effects=True),
    )(field, link, source_z, displacements, momenta, gamma_perm, gamma_phase)
    used = reduced.reshape(nta, lane_rows * LANES)[:, : ndisp * ng * np_ * 2]
    return jnp.swapaxes(used.reshape(nta, ndisp, ng, 2, np_), 3, 4)


def solution(mesh):
    placed = (
        P(None, None, None, None, "ta", "gz", "gy"),
        P(None, None, None, "ta", "gz", "gy"),
        P(),
        P(),
        P(),
        P(),
        P(),
    )
    ranks = tuple(mesh.shape[axis] for axis in ("ta", "gz", "gy"))
    return jax.shard_map(
        functools.partial(body, ranks), mesh=mesh, in_specs=placed, out_specs=P(), check_vma=False
    )
```

time: 51.7 us -> 16.8 us (0.32)
  blocking collectives: 39.7 us -> 0 us
  Pallas kernels: 0 us -> 15.3 us
  other arithmetic: 2.84 us -> 0 us
  local copies, waits for them, and re-layouts: 4.07 us -> 1.37 us
  starting transfers between devices: 2.43 us -> 0 us
  matrix products: 2.18 us -> 0 us
    psum x1 -> x0, blocking collectives: 39.7 us -> none  [body(): return lax.psum(ordered, ('ta', 'gz', 'gy'))]
    pallas_call x0 -> x1, Pallas kernels: none -> 15.3 us  [body(): pl.pallas_call(functools.partial(kernel, sizes, scaling, ranks), out_shap...]
    unnamed x10 -> x2, local copies, waits for them, and re-layouts: 3.31 us -> 0.65 us
    ppermute x1 -> x0, starting transfers between devices: 2.43 us -> none  [from_behind(): lax.ppermute(array, axis, [(i, (i + by) % peers) for i in range(peers)])]
    dot_general x13 -> x0, matrix products: 2.18 us -> none  [the longest x12 1.96 us: contract(): jnp.einsum('tl,gl,pl->tgp', slice_weight, trace, table, precision=highest)]
    convert_element_type x4 -> x0, other arithmetic: 1.61 us -> none  [the longest x1 0.9 us: body(): source = field_flat.astype(jnp.float32)]
    reduce_sum x5 -> x0, other arithmetic: 0.91 us -> none  [the longest x1 0.4 us: spin_pairs(): jnp.sum(source_real * field_real + source_imag * field_imag, axis=(2, 3))]
    reshape x0 -> x1, local copies, waits for them, and re-layouts: none -> 0.72 us  [body(): return jnp.swapaxes(used.reshape(nta, ndisp, ng, 2, np_), 3, 4)]
  transfers between devices with their start and end apart: 1 -> 0, of which waited for: 0 -> 0; matrix products, arithmetic and copies ran while one was open for 4% -> 0% of each run, Pallas kernels for 0% -> 0%
where the time goes in v1:
time: 16.8 us; the launch traced here: 16.7 us
  Pallas kernels  15.3 us (91%)
  local copies, waits for them, and re-layouts  1.37 us (8%)
    pallas_call x1, Pallas kernels, body(): pl.pallas_call(functools.partial(kernel, sizes, scaling, ranks), out_shap...  15.3 us
    reshape x1, local copies, waits for them, and re-layouts, body(): return jnp.swapaxes(used.reshape(nta, ndisp, ng, 2, np_), 3, 4)  0.72 us
    unnamed x2, local copies, waits for them, and re-layouts  0.65 us

profile of v1, /device:TPU:0, one launch (start us, length us, event | category | flops | bytes accessed | tf_op | source)
XLA Modules:
  0.0 16.7 jit_solution(3037487494680116349)
XLA Ops:
  0.0 15.3 %shard_map.73 = f32[2,1,128]{2,1,0:T(1,128)} custom-call(bf16[288,128]{1,0:T(8,128)(2,1)} %bitcast.9, bf16[9,2,128]{2,1,0:T(2,128)(2,1)} %bitcast.10, s32[2,4]{1,0:T(2,128)} %src_h.1, s32[3]{0:T(128)} %disp_h.1, s32[4]{0:T(128)} %mom_h.1, s32[4,4]{1,0:T(4,128)} %perm_h.1, s32[4,4]{1,0:T(4,128)} %phase_h.1), custom_call_target="tpu_custom_call" | custom-call | tf_op jit(solution)/shard_map/pallas_call | solution.py:244
  15.3 0.0 copy-start
  15.3 0.7 %copy-done = f32[2,1,128]{2,1,0:T(1,128)S(1)} copy-done((f32[2,1,128]{2,1,0:T(1,128)S(1)}, f32[2,1,128]{2,1,0:T(1,128)}, u32[]{:S(2)}) %copy-start) | copy-done | bytes 1048
  16.0 0.7 %reshape.15 = f32[2,3,4,2,4]{4,3,2,1,0:T(2,128)} reshape(f32[2,96]{1,0:T(2,128)S(1)} %bitcast.11) | data formatting | bytes 1536 | tf_op jit(solution)/shard_map/reshape | solution.py:269
Async XLA Ops:
  15.3 0.7 %copy-start = (f32[2,1,128]{2,1,0:T(1,128)S(1)}, f32[2,1,128]{2,1,0:T(1,128)}, u32[]{:S(2)}) copy-start(f32[2,1,128]{2,1,0:T(1,128)} %shard_map.73) | copy-start | bytes 3076

commit v2 on v1

--- a/solution.py
+++ b/solution.py
@@ -89,8 +89,8 @@
     out,
     near, near_links, far, far_links, left, right,
     src, disp, mom, perm, phase,
-    stage1, stage2,
-    local_sem, s_send, s_recv, u_send, u_recv, a_send, a_recv, b_send, b_recv,
+    gathered, result,
+    local_sem, s_send, s_recv, u_send, u_recv, a_send, a_recv,
 ):
     ndisp, ng, np_, nz = sizes
     nta, ngz, ngy = ranks
@@ -98,8 +98,9 @@
     rows = near.shape[0]
     part_rows = rows // 2
     colour_rows = part_rows // 3
-    lane_rows = stage1.shape[1]
+    lane_rows = gathered.shape[1]
     ta, gz, gy = lax.axis_index("ta"), lax.axis_index("gz"), lax.axis_index("gy")
+    place = (ta * ngz + gz) * ngy + gy
 
     loads = [
         pltpu.make_async_copy(a, b, local_sem.at[i])
@@ -111,15 +112,21 @@
     for load in loads:
         load.start()
 
+    def peer(step):
+        across = lax.rem(step // (ngy * ngz) + ta, nta)
+        along = lax.rem(lax.rem(step, ngz) + gz, ngz)
+        beside = lax.rem(lax.rem(step // ngz, ngy) + gy, ngy)
+        return (across, along, beside)
+
     barrier = pltpu.get_barrier_semaphore()
-    peers1 = [(ta, lax.rem(gz + d, ngz), gy) for d in range(1, ngz)]
-    peers2 = [
-        (lax.rem(ta + i, nta), gz, lax.rem(gy + j, ngy))
-        for i in range(nta) for j in range(ngy) if i + j
-    ]
-    for peer in peers1 + peers2:
-        pl.semaphore_signal(barrier, inc=1, device_id=peer, device_id_type=MESH)
-    pl.semaphore_wait(barrier, len(peers1) + len(peers2))
+    each(
+        ranks,
+        lambda step: pl.semaphore_signal(
+            barrier, inc=1, device_id=peer(step), device_id_type=MESH
+        ),
+    )
+    count = nta * ngz * ngy
+    pl.semaphore_wait(barrier, count - 1)
 
     loads[0].wait()
     loads[1].wait()
@@ -197,35 +204,39 @@
         chosen = jnp.zeros(table.shape, jnp.float32)
         for k in range(nsteps + 1):
             chosen = jnp.where(reach == k, sums[k], chosen)
-        stage1[gz, pl.ds(h, 1), :] = jnp.sum(chosen * table, axis=0, keepdims=True)
-
-    first = []
-    for d in range(1, ngz):
-        first.append(pltpu.make_async_remote_copy(
-            src_ref=stage1.at[gz], dst_ref=stage1.at[gz], send_sem=a_send.at[d],
-            recv_sem=a_recv.at[d], device_id=peers1[d - 1], device_id_type=MESH))
-        first[-1].start()
-    for copy in first:
-        copy.wait_recv()
-    total = stage1[0]
-    for d in range(1, ngz):
-        total = total + stage1[d]
-    stage2[ta, gy] = total
-    second = []
-    for d, peer in enumerate(peers2):
-        second.append(pltpu.make_async_remote_copy(
-            src_ref=stage2.at[ta, gy], dst_ref=stage2.at[ta, gy], send_sem=b_send.at[d],
-            recv_sem=b_recv.at[d], device_id=peer, device_id_type=MESH))
-        second[-1].start()
-    for copy in second:
-        copy.wait_recv()
+        gathered[place, pl.ds(h, 1), :] = jnp.sum(chosen * table, axis=0, keepdims=True)
+
+    each(
+        ranks,
+        lambda step: pltpu.make_async_remote_copy(
+            src_ref=gathered.at[place], dst_ref=gathered.at[place], send_sem=a_send.at[0],
+            recv_sem=a_recv.at[0], device_id=peer(step), device_id_type=MESH).start(),
+    )
+    others = gathered.at[pl.ds(0, count - 1)]
+    pltpu.make_async_copy(others, others, a_recv.at[0]).wait()
     for t in range(nta):
-        total = stage2[t, 0]
-        for d in range(1, ngy):
-            total = total + stage2[t, d]
-        out[t] = total
-    for copy in sends + link_sends + first + second:
+        block = gathered[pl.ds(t * ngz * ngy, ngz * ngy)]
+        result[t] = jnp.sum(block, axis=0)
+    done = pltpu.make_async_copy(result, out, local_sem.at[7])
+    done.start()
+    for copy in sends + link_sends:
         copy.wait_send()
+    pltpu.make_async_copy(others, others, a_send.at[0]).wait()
+    done.wait()
+
+
+def each(ranks, act):
+    nta, ngz, ngy = ranks
+    count = nta * ngz * ngy
+    if count > 64:
+        lax.fori_loop(1, count, lambda step, carry: (act(step), carry)[1], 0)
+        return
+    for beside in (*range(1, ngy), 0):
+        for across in range(nta - 1, -1, -1):
+            for along in range(ngz):
+                step = (across * ngy + beside) * ngz + along
+                if step:
+                    act(step)
 
 
 def body(ranks, propagator, links, source_z, displacements, momenta, gamma_perm, gamma_phase):
@@ -244,8 +255,8 @@
     reduced = pl.pallas_call(
         functools.partial(kernel, sizes, scaling, ranks),
         out_shape=jax.ShapeDtypeStruct((nta, lane_rows, LANES), jnp.float32),
-        in_specs=[pl.BlockSpec(memory_space=pl.ANY)] * 7,
-        out_specs=pl.BlockSpec(memory_space=pltpu.VMEM),
+        in_specs=[pl.BlockSpec(memory_space=pltpu.HBM)] * 7,
+        out_specs=pl.BlockSpec(memory_space=pl.ANY),
         scratch_shapes=[
             pltpu.VMEM((rows, sites), jnp.bfloat16),
             pltpu.VMEM((9, 2, sites), jnp.bfloat16),
@@ -258,12 +269,12 @@
             pltpu.SMEM(momenta.shape, jnp.int32),
             pltpu.SMEM(gamma_perm.shape, jnp.int32),
             pltpu.SMEM(gamma_phase.shape, jnp.int32),
-            pltpu.VMEM((ngz, lane_rows, LANES), jnp.float32),
-            pltpu.VMEM((nta, ngy, lane_rows, LANES), jnp.float32),
-            dma((7,)), dma((nsteps,)), dma((nsteps,)), dma((more,)), dma((more,)),
-            dma((ngz,)), dma((ngz,)), dma((nta * ngy,)), dma((nta * ngy,)),
+            pltpu.VMEM((nta * ngz * ngy, lane_rows, LANES), jnp.float32),
+            pltpu.VMEM((nta, lane_rows, LANES), jnp.float32),
+            dma((8,)), dma((nsteps,)), dma((nsteps,)), dma((more,)), dma((more,)),
+            dma((1,)), dma((1,)),
         ],
-        compiler_params=pltpu.CompilerParams(collective_id=0, has_side_effects=True),
+        compiler_params=pltpu.CompilerParams(collective_id=0, has_side_effects=True, vmem_limit_bytes=8 << 20),
     )(field, link, source_z, displacements, momenta, gamma_perm, gamma_phase)
     used = reduced.reshape(nta, lane_rows * LANES)[:, : ndisp * ng * np_ * 2]
     return jnp.swapaxes(used.reshape(nta, ndisp, ng, 2, np_), 3, 4)

time: 16.8 us -> 17.6 us (1.048)
  local copies, waits for them, and re-layouts: 1.37 us -> 4.32 us
  Pallas kernels: 15.3 us -> 13.1 us
    unnamed x2 -> x14, local copies, waits for them, and re-layouts: 0.65 us -> 3.6 us
    pallas_call x1, Pallas kernels: 15.3 us -> 13.1 us  [body(): pl.pallas_call(functools.partial(kernel, sizes, scaling, ranks), out_shap...]
where the time goes in v2:
time: 17.6 us; the launch traced here: 17.4 us
  Pallas kernels  13.1 us (74%)
  local copies, waits for them, and re-layouts  4.32 us (25%)
    pallas_call x1, Pallas kernels, body(): pl.pallas_call(functools.partial(kernel, sizes, scaling, ranks), out_shap...  13.1 us
    unnamed x14, local copies, waits for them, and re-layouts  3.6 us
    reshape x1, local copies, waits for them, and re-layouts, body(): return jnp.swapaxes(used.reshape(nta, ndisp, ng, 2, np_), 3, 4)  0.72 us

profile of v2, /device:TPU:0, one launch (start us, length us, event | category | flops | bytes accessed | tf_op | source)
XLA Modules:
  0.0 17.4 jit_solution(17892089864642226567)
XLA Ops:
  0.0 0.0 copy-start.2
  0.0 0.0 copy-start.4
  0.0 0.0 copy-start.5
  0.0 0.7 %copy-done.2 = s32[4,4]{1,0:T(4,128)S(1)} copy-done((s32[4,4]{1,0:T(4,128)S(1)}, s32[4,4]{1,0:T(4,128)}, u32[]{:S(2)}) %copy-start.2) | copy-done | bytes 88
  0.7 0.0 copy-done.4
  0.7 0.0 copy-done.5
  0.7 0.0 copy-start
  0.7 0.9 %copy-done = bf16[2,4,3,12,1,1,128]{6,1,5,4,3,2,0:T(4,128)(2,1)S(1)} copy-done((bf16[2,4,3,12,1,1,128]{6,1,5,4,3,2,0:T(4,128)(2,1)S(1)}, bf16[2,4,3,12,1,1,128]{6,1,5,4,3,2,0:T(4,128)(2,1)}, u32[]{:S(2)}) %copy-start) | copy-done | bytes 73752
  1.6 0.0 copy-start.1
  1.6 0.7 %copy-done.1 = bf16[2,3,3,1,1,128]{5,0,4,3,2,1:T(2,128)(2,1)S(1)} copy-done((bf16[2,3,3,1,1,128]{5,0,4,3,2,1:T(2,128)(2,1)S(1)}, bf16[2,3,3,1,1,128]{5,0,4,3,2,1:T(2,128)(2,1)}, u32[]{:S(2)}) %copy-start.1) | copy-done | bytes 4632
  2.3 0.0 copy-start.3
  2.3 0.7 %copy-done.3 = s32[4,4]{1,0:T(4,128)S(1)} copy-done((s32[4,4]{1,0:T(4,128)S(1)}, s32[4,4]{1,0:T(4,128)}, u32[]{:S(2)}) %copy-start.3) | copy-done | bytes 88
  3.0 0.0 copy-start.6
  3.0 0.7 %copy-done.6 = s32[4]{0:T(128)S(1)} copy-done((s32[4]{0:T(128)S(1)}, s32[4]{0:T(128)}, u32[]{:S(2)}) %copy-start.6) | copy-done | bytes 40
  3.6 13.1 %shard_map.73 = f32[2,1,128]{2,1,0:T(1,128)S(1)} custom-call(bf16[288,128]{1,0:T(8,128)(2,1)S(1)} %bitcast.9, bf16[9,2,128]{2,1,0:T(2,128)(2,1)S(1)} %bitcast.10, s32[2,4]{1,0:T(2,128)S(1)} %copy-done.4, s32[3]{0:T(128)S(1)} %copy-done.5, s32[4]{0:T(128)S(1)} %copy-done.6, s32[4,4]{1,0:T(4,128)S(1)} %copy-done.2, s32[4,4]{1,0:T(4,128)S(1)} %copy-done.3), custom_call_target="tpu_custom_call" | custom-call | tf_op jit(solution)/shard_map/pallas_call | solution.py:255
  16.7 0.7 %reshape.15 = f32[2,3,4,2,4]{4,3,2,1,0:T(2,128)} reshape(f32[2,96]{1,0:T(2,128)S(1)} %bitcast.11) | data formatting | bytes 1536 | tf_op jit(solution)/shard_map/reshape | solution.py:280
Async XLA Ops:
  0.0 0.7 %copy-start.2 = (s32[4,4]{1,0:T(4,128)S(1)}, s32[4,4]{1,0:T(4,128)}, u32[]{:S(2)}) copy-start(s32[4,4]{1,0:T(4,128)} %perm_h.1) | copy-start | bytes 196
  0.0 0.7 %copy-start.4 = (s32[2,4]{1,0:T(2,128)S(1)}, s32[2,4]{1,0:T(2,128)}, u32[]{:S(2)}) copy-start(s32[2,4]{1,0:T(2,128)} %src_h.1) | copy-start | bytes 100
  0.0 0.7 %copy-start.5 = (s32[3]{0:T(128)S(1)}, s32[3]{0:T(128)}, u32[]{:S(2)}) copy-start(s32[3]{0:T(128)} %disp_h.1) | copy-start | bytes 40
  0.7 0.9 %copy-start = (bf16[2,4,3,12,1,1,128]{6,1,5,4,3,2,0:T(4,128)(2,1)S(1)}, bf16[2,4,3,12,1,1,128]{6,1,5,4,3,2,0:T(4,128)(2,1)}, u32[]{:S(2)}) copy-start(bf16[2,4,3,12,1,1,128]{6,1,5,4,3,2,0:T(4,128)(2,1)} %param.7) | copy-start | bytes 221188
  1.6 0.7 %copy-start.1 = (bf16[2,3,3,1,1,128]{5,0,4,3,2,1:T(2,128)(2,1)S(1)}, bf16[2,3,3,1,1,128]{5,0,4,3,2,1:T(2,128)(2,1)}, u32[]{:S(2)}) copy-start(bf16[2,3,3,1,1,128]{5,0,4,3,2,1:T(2,128)(2,1)} %param.8) | copy-start | bytes 13828
  2.3 0.7 %copy-start.3 = (s32[4,4]{1,0:T(4,128)S(1)}, s32[4,4]{1,0:T(4,128)}, u32[]{:S(2)}) copy-start(s32[4,4]{1,0:T(4,128)} %phase_h.1) | copy-start | bytes 196
  3.0 0.7 %copy-start.6 = (s32[4]{0:T(128)S(1)}, s32[4]{0:T(128)}, u32[]{:S(2)}) copy-start(s32[4]{0:T(128)} %mom_h.1) | copy-start | bytes 52

commit v3 on v2

--- a/solution.py
+++ b/solution.py
@@ -89,7 +89,7 @@
     out,
     near, near_links, far, far_links, left, right,
     src, disp, mom, perm, phase,
-    gathered, result,
+    gathered,
     local_sem, s_send, s_recv, u_send, u_recv, a_send, a_recv,
 ):
     ndisp, ng, np_, nz = sizes
@@ -181,22 +181,23 @@
                 ]
                 for a in range(3)
             ]
-        sends[k - 1].wait_recv()
         for chunk in range(colour_rows // 16):
             field = [
                 [
-                    far[k - 1, pl.ds(part * part_rows + b * colour_rows + chunk * 16, 16), :]
+                    near[pl.ds(part * part_rows + a * colour_rows + chunk * 16, 16), :]
                     .astype(jnp.float32).reshape(2, 8, LANES)
-                    for b in range(3)
+                    for a in range(3)
                 ]
                 for part in range(2)
             ]
-            for a in range(3):
-                real = sum(wilson[a][b][0] * field[0][b] - wilson[a][b][1] * field[1][b] for b in range(3))
-                imag = sum(wilson[a][b][0] * field[1][b] + wilson[a][b][1] * field[0][b] for b in range(3))
-                at = a * colour_rows + chunk * 16
-                right[pl.ds(at, 16), :] = real.reshape(16, LANES)
-                right[pl.ds(part_rows + at, 16), :] = imag.reshape(16, LANES)
+            for b in range(3):
+                real = sum(field[0][a] * wilson[a][b][0] + field[1][a] * wilson[a][b][1] for a in range(3))
+                imag = sum(field[1][a] * wilson[a][b][0] - field[0][a] * wilson[a][b][1] for a in range(3))
+                at = b * colour_rows + chunk * 16
+                left[pl.ds(at, 16), :] = real.reshape(16, LANES)
+                left[pl.ds(part_rows + at, 16), :] = imag.reshape(16, LANES)
+        sends[k - 1].wait_recv()
+        right[...] = far[k - 1].astype(jnp.float32)
         sums.append(pair_sums(left, right, rows))
 
     for h in range(lane_rows):
@@ -216,13 +217,10 @@
     pltpu.make_async_copy(others, others, a_recv.at[0]).wait()
     for t in range(nta):
         block = gathered[pl.ds(t * ngz * ngy, ngz * ngy)]
-        result[t] = jnp.sum(block, axis=0)
-    done = pltpu.make_async_copy(result, out, local_sem.at[7])
-    done.start()
+        out[t] = jnp.sum(block, axis=0)
     for copy in sends + link_sends:
         copy.wait_send()
     pltpu.make_async_copy(others, others, a_send.at[0]).wait()
-    done.wait()
 
 
 def each(ranks, act):
@@ -254,9 +252,9 @@
     dma = pltpu.SemaphoreType.DMA
     reduced = pl.pallas_call(
         functools.partial(kernel, sizes, scaling, ranks),
-        out_shape=jax.ShapeDtypeStruct((nta, lane_rows, LANES), jnp.float32),
+        out_shape=pltpu.VMEM((nta, lane_rows, LANES), jnp.float32),
         in_specs=[pl.BlockSpec(memory_space=pltpu.HBM)] * 7,
-        out_specs=pl.BlockSpec(memory_space=pl.ANY),
+        out_specs=pl.BlockSpec(memory_space=pltpu.VMEM),
         scratch_shapes=[
             pltpu.VMEM((rows, sites), jnp.bfloat16),
             pltpu.VMEM((9, 2, sites), jnp.bfloat16),
@@ -270,11 +268,10 @@
             pltpu.SMEM(gamma_perm.shape, jnp.int32),
             pltpu.SMEM(gamma_phase.shape, jnp.int32),
             pltpu.VMEM((nta * ngz * ngy, lane_rows, LANES), jnp.float32),
-            pltpu.VMEM((nta, lane_rows, LANES), jnp.float32),
-            dma((8,)), dma((nsteps,)), dma((nsteps,)), dma((more,)), dma((more,)),
+            dma((7,)), dma((nsteps,)), dma((nsteps,)), dma((more,)), dma((more,)),
             dma((1,)), dma((1,)),
         ],
-        compiler_params=pltpu.CompilerParams(collective_id=0, has_side_effects=True, vmem_limit_bytes=8 << 20),
+        compiler_params=pltpu.CompilerParams(collective_id=0, has_side_effects=True),
     )(field, link, source_z, displacements, momenta, gamma_perm, gamma_phase)
     used = reduced.reshape(nta, lane_rows * LANES)[:, : ndisp * ng * np_ * 2]
     return jnp.swapaxes(used.reshape(nta, ndisp, ng, 2, np_), 3, 4)

time: 17.6 us -> 13.8 us (0.78)
  local copies, waits for them, and re-layouts: 4.32 us -> 0.72 us
  Pallas kernels: 13.1 us -> 12.9 us
    unnamed x14 -> x0, local copies, waits for them, and re-layouts: 3.6 us -> none
where the time goes in v3:
time: 13.8 us; the launch traced here: 13.6 us
  Pallas kernels  12.9 us (93%)
  local copies, waits for them, and re-layouts  0.72 us (5%)
    pallas_call x1, Pallas kernels, body(): pl.pallas_call(functools.partial(kernel, sizes, scaling, ranks), out_shap...  12.9 us
    reshape x1, local copies, waits for them, and re-layouts, body(): return jnp.swapaxes(used.reshape(nta, ndisp, ng, 2, np_), 3, 4)  0.72 us

profile of v3, /device:TPU:0, one launch (start us, length us, event | category | flops | bytes accessed | tf_op | source)
XLA Modules:
  0.0 13.6 jit_solution(17599411257887379819)
XLA Ops:
  0.0 12.9 %shard_map.73 = f32[2,1,128]{2,1,0:T(1,128)S(1)} custom-call(bf16[288,128]{1,0:T(8,128)(2,1)} %bitcast.10, bf16[9,2,128]{2,1,0:T(2,128)(2,1)} %bitcast.11, s32[2,4]{1,0:T(2,128)} %src_h.1, s32[3]{0:T(128)} %disp_h.1, s32[4]{0:T(128)} %mom_h.1, s32[4,4]{1,0:T(4,128)} %perm_h.1, s32[4,4]{1,0:T(4,128)} %phase_h.1), custom_call_target="tpu_custom_call" | custom-call | tf_op jit(solution)/shard_map/pallas_call | solution.py:253
  12.9 0.7 %reshape.15 = f32[2,3,4,2,4]{4,3,2,1,0:T(2,128)} reshape(f32[2,96]{1,0:T(2,128)S(1)} %bitcast.9) | data formatting | bytes 1536 | tf_op jit(solution)/shard_map/reshape | solution.py:277

commit v4 on v3

--- a/solution.py
+++ b/solution.py
@@ -58,46 +58,46 @@
     return value, jnp.abs(reach)
 
 
-def pair_sums(left, right, rows):
-    half = rows // 2
-    per = half // 4
-    lefts = []
-    turned = []
-    rights = []
-    for s in range(4):
-        lefts.append(left[pl.ds(s, 2 * per, stride=4), :])
-        rights.append(right[pl.ds(s, 2 * per, stride=4), :])
-        turned.append(
-            jnp.concatenate(
-                [-left[pl.ds(half + s, per, stride=4), :], left[pl.ds(s, per, stride=4), :]],
-                axis=0,
-            )
-        )
+def add_pairs(sums, left, turned, right, start, size):
+    def rows(ref, s):
+        return ref[pl.ds(start + s, size // 4, stride=4), :].reshape(-1, 8, LANES)
+
+    rights = [rows(right, u) for u in range(4)]
     out = []
-    for group in (lefts, turned):
+    for side in (left, turned):
         for s in range(4):
-            for u in range(4):
-                product = (group[s] * rights[u]).reshape(2 * per // 8, 8, LANES)
-                out.append(jnp.sum(jnp.sum(product, axis=0), axis=0, keepdims=True))
-    stacked = jnp.concatenate(out, axis=0)
+            own = rows(side, s)
+            out += [jnp.sum(own * other, axis=0) for other in rights]
+    return out if sums is None else [x + y for x, y in zip(sums, out)]
+
+
+def site_sums(sums):
+    stacked = jnp.concatenate([jnp.sum(x, axis=0, keepdims=True) for x in sums], axis=0)
     return jnp.sum(stacked, axis=1, keepdims=True)
+
+
+def keep(left, turned, at, size, real, imag):
+    real, imag = real.reshape(-1, LANES), imag.reshape(-1, LANES)
+    left[pl.ds(at, size), :] = real
+    left[pl.ds(at + size, size), :] = imag
+    if turned is not None:
+        turned[pl.ds(at, size), :] = -imag
+        turned[pl.ds(at + size, size), :] = real
 
 
 def kernel(
     sizes, scaling, ranks,
     prop, links, src_h, disp_h, mom_h, perm_h, phase_h,
     out,
-    near, near_links, far, far_links, left, right,
+    near, near_links, far, far_links, left, turned, right,
     src, disp, mom, perm, phase,
     gathered,
-    local_sem, s_send, s_recv, u_send, u_recv, a_send, a_recv,
+    local_sem, s_send, s_recv, u_send, u_recv, a_send, a_recv, line_sem, plane_sem,
 ):
     ndisp, ng, np_, nz = sizes
     nta, ngz, ngy = ranks
     nsteps = (ndisp - 1) // 2
-    rows = near.shape[0]
-    part_rows = rows // 2
-    colour_rows = part_rows // 3
+    size = near.shape[2]
     lane_rows = gathered.shape[1]
     ta, gz, gy = lax.axis_index("ta"), lax.axis_index("gz"), lax.axis_index("gy")
     place = (ta * ngz + gz) * ngy + gy
@@ -105,8 +105,9 @@
     loads = [
         pltpu.make_async_copy(a, b, local_sem.at[i])
         for i, (a, b) in enumerate(
-            [(prop, near), (links, near_links), (src_h, src), (disp_h, disp),
-             (mom_h, mom), (perm_h, perm), (phase_h, phase)]
+            [(prop.at[:, c], near.at[:, c]) for c in range(3)]
+            + [(links, near_links), (src_h, src), (disp_h, disp),
+               (mom_h, mom), (perm_h, perm), (phase_h, phase)]
         )
     ]
     for load in loads:
@@ -118,37 +119,55 @@
         beside = lax.rem(lax.rem(step // ngz, ngy) + gy, ngy)
         return (across, along, beside)
 
+    depth_peers = [functools.partial(lambda d: (ta, lax.rem(gz + d, ngz), gy), d) for d in range(1, ngz)]
+    beside_peers = [functools.partial(lambda d: (ta, gz, lax.rem(gy + d, ngy)), d) for d in range(1, ngy)]
+    across_peers = [functools.partial(lambda d: (lax.rem(ta + d, nta), gz, gy), d) for d in range(1, nta)]
+
+    def greet(semaphore, peers):
+        for at in peers:
+            pl.semaphore_signal(semaphore, inc=1, device_id=at(), device_id_type=MESH)
+
+    count = nta * ngz * ngy
     barrier = pltpu.get_barrier_semaphore()
-    each(
-        ranks,
-        lambda step: pl.semaphore_signal(
-            barrier, inc=1, device_id=peer(step), device_id_type=MESH
-        ),
-    )
-    count = nta * ngz * ngy
-    pl.semaphore_wait(barrier, count - 1)
-
-    loads[0].wait()
-    loads[1].wait()
-    sends = []
-    for k in range(1, nsteps + 1):
-        target = (ta, lax.rem(gz + ngz - k, ngz), gy)
-        sends.append(pltpu.make_async_remote_copy(
-            src_ref=near, dst_ref=far.at[k - 1], send_sem=s_send.at[k - 1],
-            recv_sem=s_recv.at[k - 1], device_id=target, device_id_type=MESH))
-        sends[-1].start()
-    link_sends = []
-    for k in range(1, nsteps):
-        target = (ta, lax.rem(gz + ngz - k, ngz), gy)
-        link_sends.append(pltpu.make_async_remote_copy(
+    greet(barrier, depth_peers + beside_peers + across_peers)
+    pl.semaphore_wait(barrier, ngz + ngy + nta - 3)
+
+    def target(k):
+        return (ta, lax.rem(gz + ngz - k, ngz), gy)
+
+    sends = [
+        [
+            pltpu.make_async_remote_copy(
+                src_ref=near.at[:, c], dst_ref=far.at[k - 1, :, c], send_sem=s_send.at[k - 1, c],
+                recv_sem=s_recv.at[k - 1, c], device_id=target(k), device_id_type=MESH)
+            for c in range(3)
+        ]
+        for k in range(1, nsteps + 1)
+    ]
+    link_sends = [
+        pltpu.make_async_remote_copy(
             src_ref=near_links, dst_ref=far_links.at[k - 1], send_sem=u_send.at[k - 1],
-            recv_sem=u_recv.at[k - 1], device_id=target, device_id_type=MESH))
-        link_sends[-1].start()
-
-    for load in loads[2:]:
+            recv_sem=u_recv.at[k - 1], device_id=target(k), device_id_type=MESH)
+        for k in range(1, nsteps)
+    ]
+    for c in range(3):
+        loads[c].wait()
+        for copies in sends:
+            copies[c].start()
+    loads[3].wait()
+    for copy in link_sends:
+        copy.start()
+    greet(line_sem.at[0], depth_peers)
+    for load in loads[4:]:
         load.wait()
-    left[...] = near[...].astype(jnp.float32)
-    sums = [pair_sums(left, left, rows)]
+
+    sums = None
+    for c in range(3):
+        keep(left, turned, 2 * size * c, size, near[0, c].astype(jnp.float32), near[1, c].astype(jnp.float32))
+        sums = add_pairs(sums, left, turned, left, 2 * size * c, 2 * size)
+    totals = [site_sums(sums)]
+    pl.semaphore_wait(line_sem.at[0], ngz - 1)
+    greet(plane_sem.at[0], across_peers)
     tables = [
         weights(h, sizes, (src, disp, mom, perm, phase), (ta, gz), scaling)
         for h in range(lane_rows)
@@ -181,11 +200,10 @@
                 ]
                 for a in range(3)
             ]
-        for chunk in range(colour_rows // 16):
+        for chunk in range(size // 16):
             field = [
                 [
-                    near[pl.ds(part * part_rows + a * colour_rows + chunk * 16, 16), :]
-                    .astype(jnp.float32).reshape(2, 8, LANES)
+                    near[part, a, pl.ds(chunk * 16, 16), :].astype(jnp.float32).reshape(2, 8, LANES)
                     for a in range(3)
                 ]
                 for part in range(2)
@@ -193,20 +211,28 @@
             for b in range(3):
                 real = sum(field[0][a] * wilson[a][b][0] + field[1][a] * wilson[a][b][1] for a in range(3))
                 imag = sum(field[1][a] * wilson[a][b][0] - field[0][a] * wilson[a][b][1] for a in range(3))
-                at = b * colour_rows + chunk * 16
-                left[pl.ds(at, 16), :] = real.reshape(16, LANES)
-                left[pl.ds(part_rows + at, 16), :] = imag.reshape(16, LANES)
-        sends[k - 1].wait_recv()
-        right[...] = far[k - 1].astype(jnp.float32)
-        sums.append(pair_sums(left, right, rows))
+                real, imag = real.reshape(16, LANES), imag.reshape(16, LANES)
+                at = 2 * size * b + chunk * 16
+                left[pl.ds(at, 16), :] = real
+                left[pl.ds(at + size, 16), :] = imag
+                turned[pl.ds(at, 16), :] = -imag
+                turned[pl.ds(at + size, 16), :] = real
+        sums = None
+        for c in range(3):
+            sends[k - 1][c].wait_recv()
+            keep(right, None, 2 * size * c, size,
+                 far[k - 1, 0, c].astype(jnp.float32), far[k - 1, 1, c].astype(jnp.float32))
+            sums = add_pairs(sums, left, turned, right, 2 * size * c, 2 * size)
+        totals.append(site_sums(sums))
 
     for h in range(lane_rows):
         table, reach = tables[h]
         chosen = jnp.zeros(table.shape, jnp.float32)
         for k in range(nsteps + 1):
-            chosen = jnp.where(reach == k, sums[k], chosen)
+            chosen = jnp.where(reach == k, totals[k], chosen)
         gathered[place, pl.ds(h, 1), :] = jnp.sum(chosen * table, axis=0, keepdims=True)
 
+    pl.semaphore_wait(plane_sem.at[0], nta - 1)
     each(
         ranks,
         lambda step: pltpu.make_async_remote_copy(
@@ -218,7 +244,7 @@
     for t in range(nta):
         block = gathered[pl.ds(t * ngz * ngy, ngz * ngy)]
         out[t] = jnp.sum(block, axis=0)
-    for copy in sends + link_sends:
+    for copy in sum(sends, []) + link_sends:
         copy.wait_send()
     pltpu.make_async_copy(others, others, a_send.at[0]).wait()
 
@@ -244,9 +270,10 @@
     nsteps = (ndisp - 1) // 2
     sizes = (ndisp, ng, np_, ngz)
     scaling = 1.0 / (24.0 * math.sqrt(sites * ngy * ngz))
-    field = jnp.transpose(propagator, (0, 2, 3, 4, 5, 1, 6)).reshape(-1, sites)
+    field = jnp.transpose(propagator, (0, 2, 3, 4, 5, 1, 6)).reshape(2, 3, -1, sites)
     link = jnp.transpose(links, (1, 2, 3, 4, 0, 5)).reshape(9, 2, sites)
-    rows = field.shape[0]
+    size = field.shape[2]
+    regular = pltpu.SemaphoreType.REGULAR
     lane_rows = -(-ndisp * ng * np_ * 2 // LANES)
     more = max(nsteps - 1, 1)
     dma = pltpu.SemaphoreType.DMA
@@ -256,20 +283,21 @@
         in_specs=[pl.BlockSpec(memory_space=pltpu.HBM)] * 7,
         out_specs=pl.BlockSpec(memory_space=pltpu.VMEM),
         scratch_shapes=[
-            pltpu.VMEM((rows, sites), jnp.bfloat16),
+            pltpu.VMEM((2, 3, size, sites), jnp.bfloat16),
             pltpu.VMEM((9, 2, sites), jnp.bfloat16),
-            pltpu.VMEM((nsteps, rows, sites), jnp.bfloat16),
+            pltpu.VMEM((nsteps, 2, 3, size, sites), jnp.bfloat16),
             pltpu.VMEM((more, 9, 2, sites), jnp.bfloat16),
-            pltpu.VMEM((rows, sites), jnp.float32),
-            pltpu.VMEM((rows, sites), jnp.float32),
+            pltpu.VMEM((6 * size, sites), jnp.float32),
+            pltpu.VMEM((6 * size, sites), jnp.float32),
+            pltpu.VMEM((6 * size, sites), jnp.float32),
             pltpu.SMEM(source_z.shape, jnp.int32),
             pltpu.SMEM(displacements.shape, jnp.int32),
             pltpu.SMEM(momenta.shape, jnp.int32),
             pltpu.SMEM(gamma_perm.shape, jnp.int32),
             pltpu.SMEM(gamma_phase.shape, jnp.int32),
             pltpu.VMEM((nta * ngz * ngy, lane_rows, LANES), jnp.float32),
-            dma((7,)), dma((nsteps,)), dma((nsteps,)), dma((more,)), dma((more,)),
-            dma((1,)), dma((1,)),
+            dma((9,)), dma((nsteps, 3)), dma((nsteps, 3)), dma((more,)), dma((more,)),
+            dma((1,)), dma((1,)), regular((1,)), regular((1,)),
         ],
         compiler_params=pltpu.CompilerParams(collective_id=0, has_side_effects=True),
     )(field, link, source_z, displacements, momenta, gamma_perm, gamma_phase)

time: 13.8 us -> 13.2 us (0.957)
  Pallas kernels: 12.9 us -> 12.4 us
    pallas_call x1, Pallas kernels: 12.9 us -> 12.4 us  [body(): pl.pallas_call(functools.partial(kernel, sizes, scaling, ranks), out_shap...]
where the time goes in v4:
time: 13.2 us; the launch traced here: 13.1 us
  Pallas kernels  12.4 us (94%)
  local copies, waits for them, and re-layouts  0.72 us (5%)
    pallas_call x1, Pallas kernels, body(): pl.pallas_call(functools.partial(kernel, sizes, scaling, ranks), out_shap...  12.4 us
    reshape x1, local copies, waits for them, and re-layouts, body(): return jnp.swapaxes(used.reshape(nta, ndisp, ng, 2, np_), 3, 4)  0.72 us

profile of v4, /device:TPU:0, one launch (start us, length us, event | category | flops | bytes accessed | tf_op | source)
XLA Modules:
  0.0 13.1 jit_solution(6086634883988753475)
XLA Ops:
  0.0 12.4 %shard_map.73 = f32[2,1,128]{2,1,0:T(1,128)S(1)} custom-call(bf16[2,3,48,128]{3,2,1,0:T(8,128)(2,1)} %bitcast.10, bf16[9,2,128]{2,1,0:T(2,128)(2,1)} %bitcast.11, s32[2,4]{1,0:T(2,128)} %src_h.1, s32[3]{0:T(128)} %disp_h.1, s32[4]{0:T(128)} %mom_h.1, s32[4,4]{1,0:T(4,128)} %perm_h.1, s32[4,4]{1,0:T(4,128)} %phase_h.1), custom_call_target="tpu_custom_call" | custom-call | tf_op jit(solution)/shard_map/pallas_call | solution.py:280
  12.4 0.7 %reshape.15 = f32[2,3,4,2,4]{4,3,2,1,0:T(2,128)} reshape(f32[2,96]{1,0:T(2,128)S(1)} %bitcast.9) | data formatting | bytes 1536 | tf_op jit(solution)/shard_map/reshape | solution.py:305

commit v5 on v4

--- a/solution.py
+++ b/solution.py
@@ -92,7 +92,7 @@
     near, near_links, far, far_links, left, turned, right,
     src, disp, mom, perm, phase,
     gathered,
-    local_sem, s_send, s_recv, u_send, u_recv, a_send, a_recv, line_sem, plane_sem,
+    local_sem, s_send, s_recv, a_recv, line_sem, plane_sem, *link_sems,
 ):
     ndisp, ng, np_, nz = sizes
     nta, ngz, ngy = ranks
@@ -105,20 +105,13 @@
     loads = [
         pltpu.make_async_copy(a, b, local_sem.at[i])
         for i, (a, b) in enumerate(
-            [(prop.at[:, c], near.at[:, c]) for c in range(3)]
-            + [(links, near_links), (src_h, src), (disp_h, disp),
-               (mom_h, mom), (perm_h, perm), (phase_h, phase)]
+            [(prop, near), (links, near_links), (src_h, src), (disp_h, disp),
+             (mom_h, mom), (perm_h, perm), (phase_h, phase)]
         )
     ]
     for load in loads:
         load.start()
 
-    def peer(step):
-        across = lax.rem(step // (ngy * ngz) + ta, nta)
-        along = lax.rem(lax.rem(step, ngz) + gz, ngz)
-        beside = lax.rem(lax.rem(step // ngz, ngy) + gy, ngy)
-        return (across, along, beside)
-
     depth_peers = [functools.partial(lambda d: (ta, lax.rem(gz + d, ngz), gy), d) for d in range(1, ngz)]
     beside_peers = [functools.partial(lambda d: (ta, gz, lax.rem(gy + d, ngy)), d) for d in range(1, ngy)]
     across_peers = [functools.partial(lambda d: (lax.rem(ta + d, nta), gz, gy), d) for d in range(1, nta)]
@@ -138,27 +131,28 @@
     sends = [
         [
             pltpu.make_async_remote_copy(
-                src_ref=near.at[:, c], dst_ref=far.at[k - 1, :, c], send_sem=s_send.at[k - 1, c],
+                src_ref=near.at[:, c], dst_ref=far.at[k - 1, :, c], send_sem=s_send.at[0],
                 recv_sem=s_recv.at[k - 1, c], device_id=target(k), device_id_type=MESH)
             for c in range(3)
         ]
         for k in range(1, nsteps + 1)
     ]
+    u_send, u_recv = link_sems if link_sems else (None, None)
     link_sends = [
         pltpu.make_async_remote_copy(
             src_ref=near_links, dst_ref=far_links.at[k - 1], send_sem=u_send.at[k - 1],
             recv_sem=u_recv.at[k - 1], device_id=target(k), device_id_type=MESH)
         for k in range(1, nsteps)
     ]
+    loads[0].wait()
     for c in range(3):
-        loads[c].wait()
         for copies in sends:
             copies[c].start()
-    loads[3].wait()
+    loads[1].wait()
     for copy in link_sends:
         copy.start()
     greet(line_sem.at[0], depth_peers)
-    for load in loads[4:]:
+    for load in loads[2:]:
         load.wait()
 
     sums = None
@@ -233,34 +227,41 @@
         gathered[place, pl.ds(h, 1), :] = jnp.sum(chosen * table, axis=0, keepdims=True)
 
     pl.semaphore_wait(plane_sem.at[0], nta - 1)
+    pltpu.make_async_copy(far, far, s_send.at[0]).wait()
     each(
         ranks,
-        lambda step: pltpu.make_async_remote_copy(
-            src_ref=gathered.at[place], dst_ref=gathered.at[place], send_sem=a_send.at[0],
-            recv_sem=a_recv.at[0], device_id=peer(step), device_id_type=MESH).start(),
+        place,
+        lambda at: pltpu.make_async_remote_copy(
+            src_ref=gathered.at[place], dst_ref=gathered.at[place], send_sem=s_send.at[0],
+            recv_sem=a_recv.at[0], device_id=at, device_id_type=MESH).start(),
     )
     others = gathered.at[pl.ds(0, count - 1)]
     pltpu.make_async_copy(others, others, a_recv.at[0]).wait()
     for t in range(nta):
         block = gathered[pl.ds(t * ngz * ngy, ngz * ngy)]
         out[t] = jnp.sum(block, axis=0)
-    for copy in sum(sends, []) + link_sends:
+    for copy in link_sends:
         copy.wait_send()
-    pltpu.make_async_copy(others, others, a_send.at[0]).wait()
-
-
-def each(ranks, act):
+    pltpu.make_async_copy(others, others, s_send.at[0]).wait()
+
+
+def each(ranks, place, act):
     nta, ngz, ngy = ranks
     count = nta * ngz * ngy
+
+    def one(step, along):
+        beside = step // (nta * ngz)
+        across = step // ngz % nta
+
+        @pl.when(place != (across * ngz + along) * ngy + beside)
+        def _():
+            act((across, along, beside))
+
     if count > 64:
-        lax.fori_loop(1, count, lambda step, carry: (act(step), carry)[1], 0)
+        lax.fori_loop(0, count, lambda step, carry: (one(step, step % ngz), carry)[1], 0)
         return
-    for beside in (*range(1, ngy), 0):
-        for across in range(nta - 1, -1, -1):
-            for along in range(ngz):
-                step = (across * ngy + beside) * ngz + along
-                if step:
-                    act(step)
+    for step in range(count):
+        one(step, step % ngz)
 
 
 def body(ranks, propagator, links, source_z, displacements, momenta, gamma_perm, gamma_phase):
@@ -296,9 +297,9 @@
             pltpu.SMEM(gamma_perm.shape, jnp.int32),
             pltpu.SMEM(gamma_phase.shape, jnp.int32),
             pltpu.VMEM((nta * ngz * ngy, lane_rows, LANES), jnp.float32),
-            dma((9,)), dma((nsteps, 3)), dma((nsteps, 3)), dma((more,)), dma((more,)),
-            dma((1,)), dma((1,)), regular((1,)), regular((1,)),
-        ],
+            dma((7,)), dma((1,)), dma((nsteps, 3)),
+            dma((1,)), regular((1,)), regular((1,)),
+        ] + [dma((nsteps - 1,))] * (2 if nsteps > 1 else 0),
         compiler_params=pltpu.CompilerParams(collective_id=0, has_side_effects=True),
     )(field, link, source_z, displacements, momenta, gamma_perm, gamma_phase)
     used = reduced.reshape(nta, lane_rows * LANES)[:, : ndisp * ng * np_ * 2]

time: 13.2 us -> 13.2 us (level)
  no operation moved by 1% of the time
where the time goes in v5:
time: 13.2 us; the launch traced here: 13 us
  Pallas kernels  12.3 us (93%)
  local copies, waits for them, and re-layouts  0.72 us (5%)
    pallas_call x1, Pallas kernels, body(): pl.pallas_call(functools.partial(kernel, sizes, scaling, ranks), out_shap...  12.3 us
    reshape x1, local copies, waits for them, and re-layouts, body(): return jnp.swapaxes(used.reshape(nta, ndisp, ng, 2, np_), 3, 4)  0.72 us

profile of v5, /device:TPU:0, one launch (start us, length us, event | category | flops | bytes accessed | tf_op | source)
XLA Modules:
  0.0 13.0 jit_solution(17325010067072506363)
XLA Ops:
  0.0 12.3 %shard_map.73 = f32[2,1,128]{2,1,0:T(1,128)S(1)} custom-call(bf16[2,3,48,128]{3,2,1,0:T(8,128)(2,1)} %bitcast.10, bf16[9,2,128]{2,1,0:T(2,128)(2,1)} %bitcast.11, s32[2,4]{1,0:T(2,128)} %src_h.1, s32[3]{0:T(128)} %disp_h.1, s32[4]{0:T(128)} %mom_h.1, s32[4,4]{1,0:T(4,128)} %perm_h.1, s32[4,4]{1,0:T(4,128)} %phase_h.1), custom_call_target="tpu_custom_call" | custom-call | tf_op jit(solution)/shard_map/pallas_call | solution.py:281
  12.3 0.7 %reshape.15 = f32[2,3,4,2,4]{4,3,2,1,0:T(2,128)} reshape(f32[2,96]{1,0:T(2,128)S(1)} %bitcast.9) | data formatting | bytes 1536 | tf_op jit(solution)/shard_map/reshape | solution.py:306
